TPU v7x, 32 devices: a whole 2x2x4 slice. The times are simulated.
32 devices in a mesh: seq: 16 (over z, x, core), head: 2 (over y).
Axes of the slice: x: 2, y: 2, z: 4, core: 2. Of those that a mesh axis runs over, the one named last changes fastest.
Arguments:
- tokens: bfloat16 [8192, 1024], P('seq'), may hold values from -6 to 6
- mem_query_w: bfloat16 [1024, 1024], P(None, 'head'), may hold values from -0.1875 to 0.1875
- mem_key_w: bfloat16 [1024, 1024], P(None, 'head'), may hold values from -0.1875 to 0.1875
- mem_value_w: bfloat16 [1024, 1024], P(None, 'head'), may hold values from -0.1875 to 0.1875
- mem_in: float32 [1024, 1024], P(None, 'head'), may hold values from -0.1875 to 0.1875
- mem_out: float32 [1024, 1024], P('head'), may hold values from -0.1875 to 0.1875
- forget_levels: float32 [16, 1024], P(None, 'head'), may hold values from 0.003 to 0.3
- momentum_levels: float32 [16, 1024], P(None, 'head'), may hold values from 0.2 to 0.9
- step_levels: float32 [16, 1024], P(None, 'head'), may hold values from 0.02 to 0.2
- plan: int32 [16], P('seq'), may hold values from 0 to 15
- norm_gain: float32 [1024], replicated, may hold values from 0.5 to 1.5
- attn_query_w: bfloat16 [1024, 1024], P(None, 'head'), may hold values from -1 to 1
- attn_key_w: bfloat16 [1024, 1024], P(None, 'head'), may hold values from -4 to 4
- attn_value_w: bfloat16 [1024, 1024], P(None, 'head'), may hold values from -0.1875 to 0.1875
- attn_out_w: bfloat16 [1024, 1024], P('head'), may hold values from -0.25 to 0.25
Outputs:
- layer_out: bfloat16 [8192, 1024], P('seq', 'head')
All inputs are finite; a program needn't handle non-finite values.
Results may differ from a plain program's by a relative error of at most 0.014.
Values may be sent and summed in bfloat16 or wider, within the bound.
A program may use at most 192 MiB of HBM per device.

v0:
```python
import functools
import math

import jax
import jax.numpy as jnp
from jax import lax
from jax.experimental import pallas as pl
from jax.experimental.pallas import tpu as pltpu
from jax.sharding import PartitionSpec as P

HEAD_DIM = 64
LANES = 2 * HEAD_DIM
SPAN = 8
MESH = pl.DeviceIdType.MESH

epsilon = 1e-06
ANY = pl.BlockSpec(memory_space=pl.ANY)
VMEM = pl.BlockSpec(memory_space=pltpu.VMEM)


def meet(axis, n):
    me = lax.axis_index(axis)
    barrier = pltpu.get_barrier_semaphore()
    for k in range(1, n):
        pl.semaphore_signal(
            barrier, inc=1, device_id={axis: lax.rem(me + k, n)}, device_id_type=MESH
        )
    pl.semaphore_wait(barrier, n - 1)


def remote(src, dst, send, recv, axis, peer):
    return pltpu.make_async_remote_copy(
        src_ref=src,
        dst_ref=dst,
        send_sem=send,
        recv_sem=recv,
        device_id={axis: peer},
        device_id_type=MESH,
    )


def part(ref, dim, index, size):
    window = pl.ds(pl.multiple_of(index * size, size), size)
    return ref.at[:, window] if dim == 1 else ref.at[window, :]


def gather_kernel(axis, n, dim, size, x_ref, o_ref, send, recv, local):
    me = lax.axis_index(axis)
    meet(axis, n)
    slot = part(o_ref, dim, me, size)
    copies = []
    for k in range(1, n):
        copy = remote(x_ref, slot, send.at[k - 1], recv.at[k - 1], axis, lax.rem(me + k, n))
        copy.start()
        copies.append(copy)
    own = pltpu.make_async_copy(x_ref, slot, local)
    own.start()
    own.wait()
    for copy in copies:
        copy.wait()


def split_kernel(axis, n, dim, size, x_ref, o_ref, send, recv, local):
    me = lax.axis_index(axis)
    meet(axis, n)
    copies = []
    for k in range(1, n):
        peer = lax.rem(me + k, n)
        copy = remote(
            part(x_ref, dim, peer, size),
            o_ref.at[me],
            send.at[k - 1],
            recv.at[k - 1],
            axis,
            peer,
        )
        copy.start()
        copies.append(copy)
    own = pltpu.make_async_copy(part(x_ref, dim, me, size), o_ref.at[me], local)
    own.start()
    own.wait()
    for copy in copies:
        copy.wait()


def comm_call(kernel, out, n, identity, x):
    return pl.pallas_call(
        kernel,
        out_shape=out,
        in_specs=[ANY],
        out_specs=ANY,
        scratch_shapes=[
            pltpu.SemaphoreType.DMA((n - 1,)),
            pltpu.SemaphoreType.DMA((n - 1,)),
            pltpu.SemaphoreType.DMA,
        ],
        compiler_params=pltpu.CompilerParams(collective_id=identity, has_side_effects=True),
    )(x)


def gather(x, axis, dim, identity):
    n = lax.axis_size(axis)
    shape = list(x.shape)
    shape[dim] *= n
    kernel = functools.partial(gather_kernel, axis, n, dim, x.shape[dim])
    return comm_call(kernel, jax.ShapeDtypeStruct(tuple(shape), x.dtype), n, identity, x)


def scatter_sum(x, axis, dim, identity):
    n = lax.axis_size(axis)
    shape = list(x.shape)
    shape[dim] //= n
    kernel = functools.partial(split_kernel, axis, n, dim, shape[dim])
    parts = comm_call(kernel, jax.ShapeDtypeStruct((n, *shape), x.dtype), n, identity, x)
    return jnp.sum(parts.astype(jnp.float32), axis=0)


def whole_sum(x, axis, identity):
    parts = gather(x, axis, 0, identity).reshape(-1, *x.shape)
    return jnp.sum(parts.astype(jnp.float32), axis=0)


def memory_kernel(
    n, grads_ref, gates_ref, first_ref, o_ref,
    came, gates, wide, stage, send, recv, send_gate, recv_gate, send_back, recv_back, local,
):
    me = lax.axis_index("seq")
    meet("seq", n)
    copies = []
    for k in range(1, n):
        peer = lax.rem(me + k, n)
        gate_copy = remote(
            gates_ref.at[peer], gates.at[me], send_gate.at[k - 1], recv_gate.at[k - 1], "seq", peer
        )
        gate_copy.start()
        copy = remote(
            grads_ref.at[peer], came.at[me], send.at[k - 1], recv.at[k - 1], "seq", peer
        )
        copy.start()
        copies += [gate_copy, copy]
    own_gates = pltpu.make_async_copy(gates_ref.at[me], gates.at[me], local.at[0])
    own_gates.start()
    own = pltpu.make_async_copy(grads_ref.at[me], came.at[me], local.at[1])
    own.start()
    own_gates.wait()
    own.wait()
    for copy in copies:
        copy.wait()

    for g in range(n):
        row = gates[g]
        for which in range(3):
            wide[which, g] = jnp.broadcast_to(row[:, which : which + 1], row.shape)

    def columns(c, carry):
        window = pl.ds(pl.multiple_of(c * 128, 128), 128)
        weight = first_ref[:, window]
        speed = jnp.zeros_like(weight)
        for g in range(n):
            stage[g, :, window] = weight.astype(jnp.bfloat16)
            if g < n - 1:
                grad = came[g, :, window].astype(jnp.float32)
                speed = wide[0, g] * speed - wide[2, g] * grad
                weight = (1.0 - wide[1, g]) * weight + speed
        return carry

    lax.fori_loop(0, first_ref.shape[1] // 128, columns, 0)

    copies = []
    for k in range(1, n):
        peer = lax.rem(me + k, n)
        copy = remote(
            stage.at[peer], o_ref.at[me], send_back.at[k - 1], recv_back.at[k - 1], "seq", peer
        )
        copy.start()
        copies.append(copy)
    own = pltpu.make_async_copy(stage.at[me], o_ref.at[me], local.at[2])
    own.start()
    own.wait()
    for copy in copies:
        copy.wait()


def evolve(grads, gates, first, identity):
    n = grads.shape[0]
    return pl.pallas_call(
        functools.partial(memory_kernel, n),
        out_shape=jax.ShapeDtypeStruct(grads.shape, jnp.bfloat16),
        in_specs=[ANY, ANY, VMEM],
        out_specs=ANY,
        scratch_shapes=[
            pltpu.VMEM(grads.shape, jnp.bfloat16),
            pltpu.VMEM(gates.shape, jnp.float32),
            pltpu.VMEM((3, *gates.shape), jnp.float32),
            pltpu.VMEM(grads.shape, jnp.bfloat16),
            *[pltpu.SemaphoreType.DMA((n - 1,))] * 6,
            pltpu.SemaphoreType.DMA((3,)),
        ],
        compiler_params=pltpu.CompilerParams(collective_id=identity, has_side_effects=True),
    )(grads, gates, first)


def attention_kernel(
    n, heads, q_ref, kv_ref, o_ref,
    q_all, kv_all, ctx, peaks, totals, q_send, q_recv, kv_send, kv_recv, ctx_send, ctx_recv, local,
):
    me = lax.axis_index("seq")
    chunk = me // heads
    head = lax.rem(me, heads)
    other = lax.rem(me + 1, n)
    rows = q_ref.shape[0]
    slots = SPAN + heads
    first_block = chunk * heads - SPAN
    my_slot = me - first_block
    my_tile = lax.rem(me, heads)

    def lanes(ref, which):
        return ref.at[:, pl.ds(pl.multiple_of(which * LANES, LANES), LANES)]

    def outgoing(k):
        peer = lax.rem(me + k, n)
        peer_chunk = peer // heads
        peer_head = lax.rem(peer, heads)
        slot = me - peer_chunk * heads + SPAN
        wanted = jnp.logical_and(slot >= 0, slot < slots)
        same = peer_chunk == chunk
        safe = jnp.where(wanted, slot, 0)
        kv_copy = remote(
            lanes(kv_ref, peer_head), kv_all.at[safe], kv_send.at[k - 1], kv_recv.at[safe], "seq", peer
        )
        q_copy = remote(
            lanes(q_ref, peer_head), q_all.at[my_tile], q_send.at[k - 1], q_recv.at[my_tile], "seq", peer
        )
        return wanted, same, kv_copy, q_copy

    meet("seq", n)
    own_kv = pltpu.make_async_copy(lanes(kv_ref, head), kv_all.at[my_slot], local.at[0])
    own_q = pltpu.make_async_copy(lanes(q_ref, head), q_all.at[my_tile], local.at[1])
    own_kv.start()
    own_q.start()
    for k in range(1, n):
        wanted, same, kv_copy, q_copy = outgoing(k)

        @pl.when(same)
        def _():
            q_copy.start()

        @pl.when(wanted)
        def _():
            kv_copy.start()

    own_kv.wait()
    own_q.wait()

    def await_kv(slot):
        block = first_block + slot

        @pl.when(jnp.logical_and(block >= 0, block != me))
        def _():
            remote(
                kv_all.at[slot], kv_all.at[slot], kv_send.at[0], kv_recv.at[slot], "seq", other
            ).wait_recv()

    row = lax.broadcasted_iota(jnp.int32, (rows, rows), 0)
    column = lax.broadcasted_iota(jnp.int32, (rows, rows), 1)
    scale = math.log2(math.e) * HEAD_DIM**-0.5

    def scored(query, slot):
        pair = kv_all[slot]
        scores = lax.dot_general(
            query, pair, (((1,), (1,)), ((), ())), preferred_element_type=jnp.float32
        ) * scale
        lane = lax.broadcasted_iota(jnp.int32, pair.shape, 1)
        values = jnp.where(lane < HEAD_DIM, jnp.ones_like(pair), pair)
        return scores, values

    def absorb(state, scores, values):
        peak, total = state
        new_peak = jnp.maximum(peak, jnp.max(scores, axis=1, keepdims=True))
        weights = jnp.exp2(scores - new_peak).astype(jnp.bfloat16)
        total = total * jnp.exp2(peak - new_peak) + jnp.dot(
            weights, values, preferred_element_type=jnp.float32
        )
        return new_peak, total

    def returned(tile):
        return remote(
            ctx.at[tile], lanes(o_ref, head), ctx_send.at[tile], ctx_recv.at[head], "seq",
            chunk * heads + tile,
        )

    def near(tile, carry):
        @pl.when(tile != my_tile)
        def _():
            remote(
                q_all.at[tile], q_all.at[tile], q_send.at[0], q_recv.at[tile], "seq", other
            ).wait_recv()

        await_kv(tile + SPAN)
        query = q_all[tile]
        scores, values = scored(query, tile + SPAN)
        scores = jnp.where(column <= row, scores, -1e30)
        peak = jnp.max(scores, axis=1, keepdims=True)
        weights = jnp.exp2(scores - peak).astype(jnp.bfloat16)
        state = (peak, jnp.dot(weights, values, preferred_element_type=jnp.float32))

        def whole(back, state):
            scores, values = scored(query, tile + SPAN - back)
            return absorb(state, scores, values)

        peak, total = lax.fori_loop(1, jnp.minimum(tile, SPAN - 1) + 1, whole, state)
        peaks[tile] = peak
        totals[tile] = total
        return carry

    def far(step, carry):
        tile = heads - 1 - step
        block = chunk * heads + tile

        @pl.when(tile < SPAN)
        def _():
            await_kv(tile)

        query = q_all[tile]

        def whole(back, state):
            scores, values = scored(query, tile + SPAN - back)
            return absorb(state, scores, values)

        state = lax.fori_loop(
            jnp.minimum(tile, SPAN - 1) + 1,
            jnp.minimum(block, SPAN - 1) + 1,
            whole,
            (peaks[tile], totals[tile]),
        )

        def oldest(back, state):
            scores, values = scored(query, tile)
            return absorb(state, jnp.where(column > row, scores, -1e30), values)

        peak, total = lax.fori_loop(0, jnp.where(block >= SPAN, 1, 0), oldest, state)
        ctx[tile] = (total / total[:, :1]).astype(jnp.bfloat16)

        @pl.when(tile != my_tile)
        def _():
            returned(tile).start()

        @pl.when(tile == my_tile)
        def _():
            pltpu.make_async_copy(ctx.at[tile], lanes(o_ref, head), local.at[2]).start()

        return carry

    lax.fori_loop(0, heads, near, 0)
    for slot in range(heads, SPAN):
        await_kv(slot)
    lax.fori_loop(0, heads, far, 0)

    pltpu.make_async_copy(ctx.at[my_tile], lanes(o_ref, head), local.at[2]).wait()
    for tile in range(heads):
        @pl.when(tile != my_tile)
        def _():
            returned(tile).wait_send()
            remote(
                ctx.at[tile], lanes(o_ref, tile), ctx_send.at[tile], ctx_recv.at[tile], "seq", other
            ).wait_recv()

    for k in range(1, n):
        wanted, same, kv_copy, q_copy = outgoing(k)

        @pl.when(same)
        def _():
            q_copy.wait_send()

        @pl.when(wanted)
        def _():
            kv_copy.wait_send()


def attend(query, pairs, identity):
    n = lax.axis_size("seq")
    rows = query.shape[0]
    heads = query.shape[1] // LANES
    return pl.pallas_call(
        functools.partial(attention_kernel, n, heads),
        out_shape=jax.ShapeDtypeStruct(query.shape, jnp.bfloat16),
        in_specs=[ANY, ANY],
        out_specs=ANY,
        scratch_shapes=[
            pltpu.VMEM((heads, rows, LANES), jnp.bfloat16),
            pltpu.VMEM((SPAN + heads, rows, LANES), jnp.bfloat16),
            pltpu.VMEM((heads, rows, LANES), jnp.bfloat16),
            pltpu.VMEM((heads, rows, 1), jnp.float32),
            pltpu.VMEM((heads, rows, LANES), jnp.float32),
            pltpu.SemaphoreType.DMA((n - 1,)),
            pltpu.SemaphoreType.DMA((heads,)),
            pltpu.SemaphoreType.DMA((n - 1,)),
            pltpu.SemaphoreType.DMA((SPAN + heads,)),
            pltpu.SemaphoreType.DMA((heads,)),
            pltpu.SemaphoreType.DMA((heads,)),
            pltpu.SemaphoreType.DMA((3,)),
        ],
        compiler_params=pltpu.CompilerParams(collective_id=identity, has_side_effects=True),
    )(query, pairs)


def silu_slope(values):
    sigmoid = jax.nn.sigmoid(values)
    return sigmoid * (1.0 + values * (1.0 - sigmoid))


def contract(left, right, left_dim, right_dim):
    return lax.dot_general(
        left,
        right,
        (((left_dim,), (right_dim,)), ((), ())),
        preferred_element_type=jnp.float32,
    )


def normalize(retrieved, norm_gain):
    mean_square = jnp.mean(retrieved * retrieved, axis=-1, keepdims=True)
    return (retrieved * lax.rsqrt(mean_square + epsilon) * norm_gain).astype(jnp.bfloat16)


def narrow(x):
    return x.astype(jnp.bfloat16)


def paired(left, right):
    depth, width = right.shape
    left, right = (a.reshape(depth, width // HEAD_DIM, HEAD_DIM) for a in (left, right))
    return jnp.concatenate([left, right], axis=2).reshape(depth, 2 * width)


def shards(
    tokens,
    mem_query_w,
    mem_key_w,
    mem_value_w,
    mem_in,
    mem_out,
    forget_levels,
    momentum_levels,
    step_levels,
    plan,
    norm_gain,
    attn_query_w,
    attn_key_w,
    attn_value_w,
    attn_out_w,
):
    tok_rows, width = tokens.shape
    n_seq = lax.axis_size("seq")
    my_seq = lax.axis_index("seq")
    hidden_units = mem_out.shape[0]
    share = hidden_units // n_seq
    key_part = narrow(contract(tokens, mem_key_w, 1, 0))
    mem_key = gather(key_part, "head", 1, 0)
    mem_query = lax.all_gather(
        narrow(contract(tokens, mem_query_w, 1, 0)), "head", axis=1, tiled=True
    )
    value_part = narrow(contract(tokens, mem_value_w, 1, 0)).astype(jnp.float32)
    pair = lax.axis_size("head") <= 2
    out_narrow = narrow(mem_out)
    pre_act = contract(mem_key, narrow(mem_in), 1, 0)
    hidden = narrow(jax.nn.silu(pre_act))
    partial = contract(hidden, out_narrow, 1, 0)
    if pair:
        mine_first = lax.axis_index("head") * value_part.shape[1]
        value_wide = lax.dynamic_update_slice_in_dim(
            jnp.zeros_like(partial), value_part, mine_first, 1
        )
        residual_err = narrow(2.0 / tok_rows * whole_sum(narrow(partial - value_wide), "head", 1))
    else:
        predicted = scatter_sum(narrow(partial), "head", 1, 1)
        residual_err = gather(narrow(2.0 / tok_rows * (predicted - value_part)), "head", 1, 2)
    grad_out = contract(hidden, residual_err, 0, 0)
    slope_term = narrow(contract(residual_err, out_narrow, 1, 1) * silu_slope(pre_act))
    grad_in = contract(slope_term, mem_key, 0, 0)
    grads = narrow(jnp.concatenate([grad_in, grad_out], axis=1)).reshape(
        n_seq, share, 2 * width
    )

    def mine(array, dim):
        return lax.dynamic_slice_in_dim(array, my_seq * share, share, dim)

    first = jnp.concatenate([mine(mem_in, 1).T, mine(mem_out, 0)], axis=1)
    matches = jnp.arange(forget_levels.shape[0], dtype=jnp.int32)[:, None] == plan[0]
    chosen = [
        jnp.sum(jnp.where(matches, table, 0.0), axis=0)
        for table in (momentum_levels, forget_levels, step_levels)
    ]
    gates = jnp.pad(jnp.stack(chosen, axis=1), ((0, 0), (0, 125))).reshape(n_seq, share, 128)
    weights = evolve(grads, gates, first, 3).reshape(hidden_units, 2 * width)
    query_hidden = narrow(jax.nn.silu(contract(mem_query, weights[:, :width], 1, 1)))
    partial = narrow(contract(query_hidden, weights[:, width:], 1, 0))
    if pair:
        normed = normalize(whole_sum(partial, "head", 4), norm_gain)
    else:
        retrieved = scatter_sum(partial, "head", 0, 4)
        normed = gather(normalize(retrieved, norm_gain), "head", 0, 5)
    query_w = paired(attn_query_w, jnp.zeros_like(attn_query_w))
    pair_w = paired(attn_key_w, attn_value_w)
    att_query = narrow(contract(normed, query_w, 1, 0))
    att_pairs = narrow(contract(normed, pair_w, 1, 0))
    context = attend(att_query, att_pairs, 6)
    heads = attn_out_w.shape[0] // HEAD_DIM
    out_rows = attn_out_w.reshape(heads, HEAD_DIM, width)
    out_w = jnp.concatenate([jnp.zeros_like(out_rows), out_rows], axis=1).reshape(
        heads * LANES, width
    )
    return narrow(scatter_sum(narrow(contract(context, out_w, 1, 0)), "head", 1, 7))


def solution(mesh):
    in_specs = (
        P("seq", None),
        P(None, "head"),
        P(None, "head"),
        P(None, "head"),
        P(None, "head"),
        P("head", None),
        P(None, "head"),
        P(None, "head"),
        P(None, "head"),
        P("seq"),
        P(),
        P(None, "head"),
        P(None, "head"),
        P(None, "head"),
        P("head", None),
    )
    out_specs = P("seq", "head")
    return jax.shard_map(shards, mesh=mesh, in_specs=in_specs, out_specs=out_specs, check_vma=False)
```

profile of v0, /device:TPU:27, one launch (start us, length us, event | category | flops | bytes accessed | tf_op | source)
XLA Modules:
  0.0 394.1 jit_solution(7765813760327539956)
XLA Ops:
  6.5 1.2 copy-done
  7.8 2.8 convolution_convert_fusion.8
  10.6 2.9 convolution_convert_fusion.7.x_ref
  13.4 18.2 %shard_map.145 = bf16[512,1024]{1,0:T(8,128)(2,1)} custom-call(bf16[512,512]{1,0:T(8,128)(2,1)} %convolution_convert_fusion.7.x_ref), custom_call_target="tpu_custom_call" | custom-call | tf_op jit(solution)/shard_map/pallas_call | solution.py:87
  31.7 2.9 fusion.14
  34.6 1.0 constant_dynamic-slice_fusion.1
  35.6 0.9 constant_dynamic-slice_fusion
  36.8 1.0 copy-done.16
  39.7 1.7 subtract_convert_fusion.x_ref
  41.4 34.7 %shard_map.146 = bf16[1024,1024]{1,0:T(8,128)(2,1)} custom-call(bf16[512,1024]{1,0:T(8,128)(2,1)} %subtract_convert_fusion.x_ref), custom_call_target="tpu_custom_call" | custom-call | tf_op jit(solution)/shard_map/pallas_call | solution.py:87
  76.1 2.3 convert_reduce_fusion.1
  78.5 1.3 copy-done.5
  79.8 1.8 convolution_convert_fusion.4
  82.5 0.7 pad_maximum_fusion.2.first_ref
  84.8 2.3 copy.26
  87.0 1.5 copy.24
  88.5 1.6 concatenate.25
  90.1 1.6 concatenate.27
  91.7 5.0 %convolution_convert_fusion.5 = bf16[512,1024]{1,0:T(8,128)(2,1)} fusion(bf16[512,1024]{1,0:T(8,128)(2,1)S(1)} %copy-done.1, f32[512,512]{1,0:T(8,128)} %fusion.14, f32[512,1024]{1,0:T(8,128)} %param.20, f32[512,1024]{1,0:T(8,128)} %copy-done.5), kind=kOutput, calls=%fused_computation.13 | convolution fusion | flops 1078198272 | bytes 7340032 | tf_op jit(solution)/shard_map/dot_general | solution.py:413
  96.7 3.1 pad_maximum_fusion.grads_ref
  99.8 113.6 %shard_map.147 = bf16[16,32,2048]{2,1,0:T(8,128)(2,1)} custom-call(bf16[16,32,2048]{2,1,0:T(8,128)(2,1)} %pad_maximum_fusion.grads_ref, f32[16,32,128]{2,1,0:T(8,128)} %bitcast.43, f32[32,2048]{1,0:T(8,128)} %pad_maximum_fusion.2.first_ref), custom_call_target="tpu_custom_call" | custom-call | tf_op jit(solution)/shard_map/pallas_call | solution.py:186
  213.4 1.6 pad_maximum_fusion.1
  215.1 4.3 %convolution_convert_fusion.3.x_ref = bf16[512,1024]{1,0:T(8,128)(2,1)} fusion(bf16[512,2048]{1,0:T(8,128)(2,1)} %bitcast.42, bf16[512,1024]{1,0:T(8,128)(2,1)} %all-gather.2.cloned.1.call-done), kind=kOutput, calls=%fused_computation.11 | convolution fusion | flops 1075576832 | bytes 4194304 | tf_op jit(solution)/shard_map/dot_general | solution.py:413
  219.3 32.9 %shard_map.148 = bf16[1024,1024]{1,0:T(8,128)(2,1)} custom-call(bf16[512,1024]{1,0:T(8,128)(2,1)} %convolution_convert_fusion.3.x_ref), custom_call_target="tpu_custom_call" | custom-call | tf_op jit(solution)/shard_map/pallas_call | solution.py:87
  252.2 2.3 convert_reduce_fusion
  254.8 1.3 copy-done.7
  256.1 2.3 convolution_convert_fusion.1.kv_ref
  258.4 2.3 convolution_convert_fusion.2.q_ref
  260.7 102.2 %shard_map.149 = bf16[512,1024]{1,0:T(8,128)(2,1)} custom-call(bf16[512,1024]{1,0:T(8,128)(2,1)} %convolution_convert_fusion.2.q_ref, bf16[512,1024]{1,0:T(8,128)(2,1)} %convolution_convert_fusion.1.kv_ref), custom_call_target="tpu_custom_call" | custom-call | tf_op jit(solution)/shard_map/pallas_call | solution.py:384
  363.0 3.5 convolution_convert_fusion.x_ref
  366.4 18.5 %shard_map.150 = bf16[2,512,512]{2,1,0:T(8,128)(2,1)} custom-call(bf16[512,1024]{1,0:T(8,128)(2,1)} %convolution_convert_fusion.x_ref), custom_call_target="tpu_custom_call" | custom-call | tf_op jit(solution)/shard_map/pallas_call | solution.py:87
  384.9 2.3 reduce_sum.72
  (46 shorter events, 4.1 us)
Async XLA Ops:
  6.5 1.2 copy-start
  6.5 208.5 %all-gather.2.cloned.1.call-start = ((), (), s32[]{:S(2)}) async-start(), calls=%async_computation | async-start | bytes 1572864 | tf_op jit(solution)/shard_map/all_gather | solution.py:460
  10.6 21.1 %copy-start.3 = (f32[1024,512]{1,0:T(8,128)S(1)}, f32[1024,512]{1,0:T(8,128)}, u32[]{:S(2)}) copy-start(f32[1024,512]{1,0:T(8,128)} %param.19) | copy-start | bytes 6291460
  36.6 1.2 copy-start.16
  37.8 1.2 copy-start.11
  37.8 1.9 copy-start.15
  78.4 1.3 copy-start.5
  79.8 1.8 copy-start.8
  79.8 3.5 copy-start.12
  79.8 3.5 copy-start.13
  79.8 3.5 copy-start.14
  81.6 2.7 copy-start.9
  88.5 1.6 copy-start.10
  90.1 1.6 copy-start.1
  99.8 113.6 %copy-start.2 = (bf16[1024,512]{0,1:T(8,128)(2,1)S(1)}, bf16[1024,512]{0,1:T(8,128)(2,1)}, u32[]{:S(2)}) copy-start(bf16[1024,512]{0,1:T(8,128)(2,1)} %copy.26) | copy-start | bytes 3145732
  254.5 1.6 copy-start.7
  254.6 1.6 copy-start.17
  256.1 2.3 copy-start.6
  260.7 102.2 %copy-start.4 = (bf16[8,128,1024]{2,1,0:T(8,128)(2,1)S(1)}, bf16[8,128,1024]{2,1,0:T(8,128)(2,1)}, u32[]{:S(2)}) copy-start(bf16[8,128,1024]{2,1,0:T(8,128)(2,1)} %concatenate.27) | copy-start | bytes 6291460
Sparse Core Ops, SparseCore 0:
  10.7 28.2 all-gather.1
where the time goes:
time: 398 us; the launch traced here: 394 us
  Pallas kernels  320 us (80%)
  matrix products  30.1 us (8%)
  local copies, waits for them, and re-layouts  16.8 us (4%)
  between operations  14.4 us (4%)
  other arithmetic  12.8 us (3%)
    pallas_call x1, Pallas kernels, evolve(): pl.pallas_call(functools.partial(memory_kernel, n), out_shape=jax.ShapeDt...  114 us
    pallas_call x4, Pallas kernels, comm_call(): pl.pallas_call(kernel, out_shape=out, in_specs=[ANY], out_specs=ANY, scra...  104 us
    pallas_call x1, Pallas kernels, attend(): pl.pallas_call(functools.partial(attention_kernel, n, heads), out_shape=j...  102 us
    dot_general x11, matrix products, contract(): lax.dot_general(left, right, (((left_dim,), (right_dim,)), ((), ())), pre...  30.1 us
    unnamed x41, local copies, waits for them, and re-layouts  10.7 us
  transfers between devices with their start and end apart: 1, of which 0 were waited for; matrix products, arithmetic and copies ran while one was open for 9% of the time, Pallas kernels for 42%

commit v1 on v0

--- a/solution.py
+++ b/solution.py
@@ -513,6 +513,272 @@
     return narrow(scatter_sum(narrow(contract(context, out_w, 1, 0)), "head", 1, 7))
 
 
+def chain_kernel(
+    n, layer, chunks, grads_ref, gates_ref, first_ref, query_ref, o_ref, other_ref,
+    came, gates, state_in, state_out, stage, current,
+    send, recv, send_gate, recv_gate, send_back, recv_back, send_z, recv_z, send_q, recv_q,
+):
+    me = lax.axis_index("seq")
+    head = lax.axis_index("head")
+    depth = me // layer
+    place = lax.rem(me, layer)
+    base = depth * layer
+    deepest = n // layer - 1
+    rows = grads_ref.shape[0] // chunks
+    up = jnp.minimum(me + layer, n - 1)
+    down = jnp.maximum(me - layer, 0)
+
+    def span(j):
+        return pl.ds(pl.multiple_of(j * rows, rows), rows)
+
+    def lanes(which):
+        return pl.ds(pl.multiple_of(which * LANES, LANES), LANES)
+
+    def mate(k):
+        return lax.rem(place + k, layer)
+
+    def gate_copy(k):
+        peer = mate(k)
+        return remote(
+            gates_ref.at[peer], gates.at[place], send_gate.at[peer], recv_gate.at[place], "seq", base + peer
+        )
+
+    def grad_copy(j, k):
+        peer = mate(k)
+        return remote(
+            grads_ref.at[span(j), lanes(peer)], came.at[j, place], send.at[j, peer], recv.at[j, place],
+            "seq", base + peer,
+        )
+
+    def back_copy(j, k):
+        peer = mate(k)
+        return remote(
+            stage.at[j, peer], o_ref.at[span(j), lanes(place)], send_back.at[j, peer], recv_back.at[j, place],
+            "seq", base + peer,
+        )
+
+    def state_copy(j):
+        return remote(state_out.at[j], state_in.at[j], send_z.at[j], recv_z.at[j], "seq", up)
+
+    query_copy = remote(query_ref, other_ref, send_q, recv_q, "head", 1 - head)
+
+    barrier = pltpu.get_barrier_semaphore()
+    for k in range(1, layer):
+        pl.semaphore_signal(barrier, inc=1, device_id={"seq": base + mate(k)}, device_id_type=MESH)
+    pl.semaphore_signal(barrier, inc=1, device_id={"head": 1 - head}, device_id_type=MESH)
+
+    @pl.when(depth < deepest)
+    def _():
+        pl.semaphore_signal(barrier, inc=1, device_id={"seq": up}, device_id_type=MESH)
+
+    @pl.when(depth > 0)
+    def _():
+        pl.semaphore_signal(barrier, inc=1, device_id={"seq": down}, device_id_type=MESH)
+
+    pl.semaphore_wait(
+        barrier, layer + jnp.where(depth < deepest, 1, 0) + jnp.where(depth > 0, 1, 0)
+    )
+
+    query_copy.start()
+    for k in range(1, layer):
+        gate_copy(k).start()
+
+    def launch(j, carry):
+        for k in range(1, layer):
+            grad_copy(j, k).start()
+        return carry
+
+    lax.fori_loop(0, chunks, launch, 0)
+    gates[place] = gates_ref[place]
+
+    def keep(j, carry):
+        came[j, place] = grads_ref[span(j), lanes(place)]
+        return carry
+
+    lax.fori_loop(0, chunks, keep, 0)
+    for k in range(1, layer):
+        peer = mate(k)
+        remote(
+            gates_ref.at[peer], gates.at[peer], send_gate.at[peer], recv_gate.at[peer], "seq", base + peer
+        ).wait_recv()
+
+    def advance(j, carry):
+        for k in range(1, layer):
+            peer = mate(k)
+            remote(
+                came.at[j, peer], came.at[j, peer], send.at[j, peer], recv.at[j, peer], "seq", base + peer
+            ).wait_recv()
+
+        @pl.when(depth > 0)
+        def _():
+            state_copy(j).wait_recv()
+            current[0] = state_in[j, 0].astype(jnp.float32)
+            current[1] = state_in[j, 1].astype(jnp.float32)
+
+        @pl.when(depth == 0)
+        def _():
+            current[0] = jnp.zeros((rows, LANES), jnp.float32)
+            current[1] = first_ref[span(j), :]
+
+        speed = current[0]
+        weight = current[1]
+        for g in range(layer):
+            stage[j, g] = weight.astype(jnp.bfloat16)
+            grad = came[j, g].astype(jnp.float32)
+            speed = gates[g, 0:1, :] * speed - gates[g, 2:3, :] * grad
+            weight = (1.0 - gates[g, 1:2, :]) * weight + speed
+        state_out[j, 0] = speed.astype(jnp.bfloat16)
+        state_out[j, 1] = weight.astype(jnp.bfloat16)
+
+        @pl.when(depth < deepest)
+        def _():
+            state_copy(j).start()
+
+        for k in range(1, layer):
+            back_copy(j, k).start()
+        o_ref[span(j), lanes(place)] = stage[j, place]
+        return carry
+
+    lax.fori_loop(0, chunks, advance, 0)
+
+    def finish(j, carry):
+        for k in range(1, layer):
+            peer = mate(k)
+            grad_copy(j, k).wait_send()
+            back_copy(j, k).wait_send()
+            remote(
+                stage.at[j, peer], o_ref.at[span(j), lanes(peer)], send_back.at[j, peer],
+                recv_back.at[j, peer], "seq", base + peer,
+            ).wait_recv()
+
+        @pl.when(depth < deepest)
+        def _():
+            state_copy(j).wait_send()
+
+        return carry
+
+    lax.fori_loop(0, chunks, finish, 0)
+    for k in range(1, layer):
+        gate_copy(k).wait_send()
+    query_copy.wait()
+
+
+def chain(grads, gates, first, query, identity):
+    n = lax.axis_size("seq")
+    layer = gates.shape[0]
+    chunks = 16
+    rows = grads.shape[0] // chunks
+    part_of = (chunks, layer, rows, LANES)
+    return pl.pallas_call(
+        functools.partial(chain_kernel, n, layer, chunks),
+        out_shape=(
+            jax.ShapeDtypeStruct(grads.shape, jnp.bfloat16),
+            jax.ShapeDtypeStruct(query.shape, jnp.bfloat16),
+        ),
+        in_specs=[VMEM, VMEM, VMEM, VMEM],
+        out_specs=(VMEM, VMEM),
+        scratch_shapes=[
+            pltpu.VMEM(part_of, jnp.bfloat16),
+            pltpu.VMEM(gates.shape, jnp.float32),
+            pltpu.VMEM((chunks, 2, rows, LANES), jnp.bfloat16),
+            pltpu.VMEM((chunks, 2, rows, LANES), jnp.bfloat16),
+            pltpu.VMEM(part_of, jnp.bfloat16),
+            pltpu.VMEM((2, rows, LANES), jnp.float32),
+            pltpu.SemaphoreType.DMA((chunks, layer)),
+            pltpu.SemaphoreType.DMA((chunks, layer)),
+            pltpu.SemaphoreType.DMA((layer,)),
+            pltpu.SemaphoreType.DMA((layer,)),
+            pltpu.SemaphoreType.DMA((chunks, layer)),
+            pltpu.SemaphoreType.DMA((chunks, layer)),
+            pltpu.SemaphoreType.DMA((chunks,)),
+            pltpu.SemaphoreType.DMA((chunks,)),
+            pltpu.SemaphoreType.DMA,
+            pltpu.SemaphoreType.DMA,
+        ],
+        compiler_params=pltpu.CompilerParams(collective_id=identity, has_side_effects=True),
+    )(grads, gates, first, query)
+
+
+def paired_shards(
+    tokens,
+    mem_query_w,
+    mem_key_w,
+    mem_value_w,
+    mem_in,
+    mem_out,
+    forget_levels,
+    momentum_levels,
+    step_levels,
+    plan,
+    norm_gain,
+    attn_query_w,
+    attn_key_w,
+    attn_value_w,
+    attn_out_w,
+):
+    tok_rows, width = tokens.shape
+    my_seq = lax.axis_index("seq")
+    my_head = lax.axis_index("head")
+    hidden_units = mem_out.shape[0]
+    layer = hidden_units // LANES
+    key_part = narrow(contract(tokens, mem_key_w, 1, 0))
+    mem_key = gather(key_part, "head", 1, 0)
+    query_part = narrow(contract(tokens, mem_query_w, 1, 0))
+    value_part = narrow(contract(tokens, mem_value_w, 1, 0)).astype(jnp.float32)
+    out_narrow = narrow(mem_out)
+    pre_act = contract(mem_key, narrow(mem_in), 1, 0)
+    hidden = narrow(jax.nn.silu(pre_act))
+    partial = contract(hidden, out_narrow, 1, 0)
+    mine_first = my_head * value_part.shape[1]
+    value_wide = lax.dynamic_update_slice_in_dim(
+        jnp.zeros_like(partial), value_part, mine_first, 1
+    )
+    residual_err = narrow(2.0 / tok_rows * whole_sum(narrow(partial - value_wide), "head", 1))
+    grad_out = contract(residual_err, hidden, 0, 0)
+    slope_term = narrow(contract(residual_err, out_narrow, 1, 1) * silu_slope(pre_act))
+    grad_in = contract(mem_key, slope_term, 0, 0)
+    grads = narrow(jnp.concatenate([grad_in, grad_out], axis=0))
+    place = lax.rem(my_seq, layer)
+
+    def mine(array, dim):
+        return lax.dynamic_slice_in_dim(array, place * LANES, LANES, dim)
+
+    first = jnp.concatenate([mine(mem_in, 1), mine(mem_out, 0).T], axis=0)
+    matches = jnp.arange(forget_levels.shape[0], dtype=jnp.int32)[:, None] == plan[0]
+    chosen = [
+        jnp.sum(jnp.where(matches, table, 0.0), axis=0)
+        for table in (momentum_levels, forget_levels, step_levels)
+    ]
+    gates = jnp.pad(jnp.stack(chosen, axis=0), ((0, 5), (0, 0)))
+    gates = gates.reshape(8, layer, LANES).transpose(1, 0, 2)
+    weights, query_other = chain(grads, gates, first, query_part, 3)
+    half = query_part.shape[1]
+    mem_query = jnp.where(
+        my_head == 0,
+        jnp.concatenate([query_part, query_other], axis=1),
+        jnp.concatenate([query_other, query_part], axis=1),
+    )
+    query_hidden = narrow(jax.nn.silu(contract(mem_query, weights[:width], 1, 0)))
+    partial = narrow(contract(query_hidden, weights[width:], 1, 1))
+    normed = normalize(whole_sum(partial, "head", 4), norm_gain)
+    query_w = paired(attn_query_w, jnp.zeros_like(attn_query_w))
+    pair_w = paired(attn_key_w, attn_value_w)
+    att_query = narrow(contract(normed, query_w, 1, 0))
+    att_pairs = narrow(contract(normed, pair_w, 1, 0))
+    context = attend(att_query, att_pairs, 6)
+    heads = attn_out_w.shape[0] // HEAD_DIM
+    out_rows = attn_out_w.reshape(heads, HEAD_DIM, width)
+    out_w = jnp.concatenate([jnp.zeros_like(out_rows), out_rows], axis=1).reshape(
+        heads * LANES, width
+    )
+    return narrow(scatter_sum(narrow(contract(context, out_w, 1, 0)), "head", 1, 7))
+
+
+def fits(n_seq, n_head, units):
+    layer = units // n_head // LANES
+    return n_head == 2 and layer * LANES * n_head == units and layer > 1 and n_seq % layer == 0
+
+
 def solution(mesh):
     in_specs = (
         P("seq", None),
@@ -532,4 +798,10 @@
         P("head", None),
     )
     out_specs = P("seq", "head")
-    return jax.shard_map(shards, mesh=mesh, in_specs=in_specs, out_specs=out_specs, check_vma=False)
+    n_seq, n_head = mesh.shape["seq"], mesh.shape["head"]
+
+    def block(*arrays):
+        body = paired_shards if fits(n_seq, n_head, arrays[4].shape[1] * n_head) else shards
+        return body(*arrays)
+
+    return jax.shard_map(block, mesh=mesh, in_specs=in_specs, out_specs=out_specs, check_vma=False)

time: 398 us -> 324 us (0.81)
  Pallas kernels: 320 us -> 260 us
  between operations: 14.4 us -> 0.9 us
    pallas_call x1, Pallas kernels: 114 us -> 54.9 us  [chain(): pl.pallas_call(functools.partial(chain_kernel, n, layer, chunks), out_sha...]
    unnamed x41 -> x38, local copies, waits for them, and re-layouts: 10.7 us -> 10.9 us
  transfers between devices with their start and end apart: 1 -> 0, of which waited for: 0 -> 0; matrix products, arithmetic and copies ran while one was open for 9% -> 0% of each run, Pallas kernels for 42% -> 0%
where the time goes in v1:
time: 324 us; the launch traced here: 321 us
  Pallas kernels  260 us (80%)
  matrix products  28.5 us (9%)
  local copies, waits for them, and re-layouts  16.3 us (5%)
  other arithmetic  14.5 us (4%)
    pallas_call x4, Pallas kernels, comm_call(): pl.pallas_call(kernel, out_shape=out, in_specs=[ANY], out_specs=ANY, scra...  103 us
    pallas_call x1, Pallas kernels, attend(): pl.pallas_call(functools.partial(attention_kernel, n, heads), out_shape=j...  103 us
    pallas_call x1, Pallas kernels, chain(): pl.pallas_call(functools.partial(chain_kernel, n, layer, chunks), out_sha...  54.9 us
    dot_general x11, matrix products, contract(): lax.dot_general(left, right, (((left_dim,), (right_dim,)), ((), ())), pre...  28.5 us
    unnamed x38, local copies, waits for them, and re-layouts  10.9 us

profile of v1, /device:TPU:27, one launch (start us, length us, event | category | flops | bytes accessed | tf_op | source)
XLA Modules:
  0.0 320.6 jit_solution(3199573362733667866)
XLA Ops:
  0.0 2.0 constant_dynamic-slice_fusion
  2.0 2.0 copy.29
  4.1 2.1 pad_maximum_fusion.2.first_ref
  6.2 1.6 broadcast_in_dim.27
  7.9 1.7 fusion.2
  9.6 1.5 convolution_convert_fusion.7.x_ref
  11.1 18.3 %shard_map.145 = bf16[512,1024]{1,0:T(8,128)(2,1)} custom-call(bf16[512,512]{1,0:T(8,128)(2,1)} %convolution_convert_fusion.7.x_ref), custom_call_target="tpu_custom_call" | custom-call | tf_op jit(solution)/shard_map/pallas_call | solution.py:87
  29.3 2.1 fusion.15
  31.4 1.0 copy-done.5
  32.4 3.3 %subtract_convert_fusion.x_ref = bf16[512,1024]{1,0:T(8,128)(2,1)} fusion(f32[512,1024]{1,0:T(8,128)} %fusion.2, f32[512,1024]{1,0:T(8,128)S(1)} %copy-done.9, f32[512,512]{1,0:T(8,128)S(1)} %fusion.15), kind=kOutput, calls=%fused_computation.7 | convolution fusion | flops 539754496 | bytes 6291456 | tf_op jit(solution)/shard_map/dot_general | solution.py:413
  35.7 33.1 %shard_map.146 = bf16[1024,1024]{1,0:T(8,128)(2,1)} custom-call(bf16[512,1024]{1,0:T(8,128)(2,1)} %subtract_convert_fusion.x_ref), custom_call_target="tpu_custom_call" | custom-call | tf_op jit(solution)/shard_map/pallas_call | solution.py:87
  68.9 3.7 %convert_reduce_fusion.1 = f32[512,1024]{1,0:T(8,128)} fusion(bf16[2,512,1024]{2,1,0:T(8,128)(2,1)} %bitcast.33), kind=kLoop, calls=%fused_computation.1 | loop fusion | flops 1572864 | bytes 4194304 | tf_op jit(solution)/shard_map/reduce_sum | solution.py:120
  72.6 4.7 %convolution_convert_fusion.5 = bf16[1024,512]{1,0:T(8,128)(2,1)} fusion(bf16[512,1024]{1,0:T(8,128)(2,1)S(1)} %copy-done.1, f32[512,512]{1,0:T(8,128)S(1)} %copy-done.6, f32[512,1024]{1,0:T(8,128)} %param.20, f32[512,1024]{1,0:T(8,128)} %convert_reduce_fusion.1), kind=kOutput, calls=%fused_computation.13 | convolution fusion | flops 1078198272 | bytes 7340032 | tf_op jit(solution)/shard_map/dot_general | solution.py:413
  77.3 2.5 convolution_convert_fusion.4
  79.9 1.4 pad_maximum_fusion.grads_ref
  82.7 1.5 convolution_convert_fusion.8.query_ref
  84.3 54.9 %shard_map.147 = (bf16[2048,512]{1,0:T(8,128)(2,1)}, bf16[512,512]{1,0:T(8,128)(2,1)}) custom-call(bf16[2048,512]{1,0:T(8,128)(2,1)} %pad_maximum_fusion.grads_ref, f32[4,8,128]{2,1,0:T(8,128)} %fusion.27.gates_ref, f32[2048,128]{1,0:T(8,128)} %pad_maximum_fusion.2.first_ref, bf16[512,512]{1,0:T(8,128)(2,1)} %convolution_convert_fusion.8.query_ref), custom_call_target="tpu_custom_call" | custom-call | tf_op jit(solution)/shard_map/pallas_call | solution.py:672
  139.1 4.3 %convolution_convert_fusion.3.x_ref = bf16[512,1024]{1,0:T(8,128)(2,1)} fusion(bf16[2048,512]{1,0:T(8,128)(2,1)} %get-tuple-element.8, bf16[512,512]{1,0:T(8,128)(2,1)} %get-tuple-element.7, bf16[512,512]{1,0:T(8,128)(2,1)S(1)} %copy-done.8, pred[]{:T(512)S(6)} %eq.14), kind=kOutput, calls=%fused_computation.11 | convolution fusion | flops 1080295424 | bytes 4194305 | tf_op jit(solution)/shard_map/dot_general | solution.py:413
  143.4 34.1 %shard_map.148 = bf16[1024,1024]{1,0:T(8,128)(2,1)} custom-call(bf16[512,1024]{1,0:T(8,128)(2,1)} %convolution_convert_fusion.3.x_ref), custom_call_target="tpu_custom_call" | custom-call | tf_op jit(solution)/shard_map/pallas_call | solution.py:87
  177.5 2.2 convert_reduce_fusion
  180.0 2.3 copy.26
  182.3 2.3 copy.27
  184.6 1.7 pad_maximum_fusion.1
  186.3 2.3 convolution_convert_fusion.1.kv_ref
  188.6 2.3 copy.25
  190.9 1.5 concatenate.26
  192.4 2.4 convolution_convert_fusion.2.q_ref
  194.8 102.7 %shard_map.149 = bf16[512,1024]{1,0:T(8,128)(2,1)} custom-call(bf16[512,1024]{1,0:T(8,128)(2,1)} %convolution_convert_fusion.2.q_ref, bf16[512,1024]{1,0:T(8,128)(2,1)} %convolution_convert_fusion.1.kv_ref), custom_call_target="tpu_custom_call" | custom-call | tf_op jit(solution)/shard_map/pallas_call | solution.py:384
  297.8 1.0 copy-done.3
  298.8 2.3 convolution_convert_fusion.x_ref
  301.0 17.2 %shard_map.150 = bf16[2,512,512]{2,1,0:T(8,128)(2,1)} custom-call(bf16[512,1024]{1,0:T(8,128)(2,1)} %convolution_convert_fusion.x_ref), custom_call_target="tpu_custom_call" | custom-call | tf_op jit(solution)/shard_map/pallas_call | solution.py:87
  318.2 2.3 reduce_sum.72
  (39 shorter events, 1.3 us)
Async XLA Ops:
  0.0 7.8 %copy-start = (bf16[512,1024]{1,0:T(8,128)(2,1)S(1)}, bf16[512,1024]{1,0:T(8,128)(2,1)}, u32[]{:S(2)}) copy-start(bf16[512,1024]{1,0:T(8,128)(2,1)} %param.15) | copy-start | bytes 3145732
  0.0 4.1 %copy-start.2 = (f32[1024,512]{1,0:T(8,128)S(1)}, f32[1024,512]{1,0:T(8,128)}, u32[]{:S(2)}) copy-start(f32[1024,512]{1,0:T(8,128)} %param.19) | copy-start | bytes 6291460
  6.2 1.6 copy-start.13
  7.8 1.7 copy-start.14
  29.3 3.1 copy-start.9
  31.4 1.0 copy-start.5
  68.9 3.7 %copy-start.1 = (bf16[512,1024]{1,0:T(8,128)(2,1)S(1)}, bf16[512,1024]{1,0:T(8,128)(2,1)}, u32[]{:S(2)}) copy-start(bf16[512,1024]{1,0:T(8,128)(2,1)} %shard_map.145) | copy-start | bytes 3145732
  68.9 3.7 %copy-start.6 = (f32[512,512]{1,0:T(8,128)S(1)}, f32[512,512]{1,0:T(8,128)}, u32[]{:S(2)}) copy-start(f32[512,512]{1,0:T(8,128)} %copy-done.5) | copy-start | bytes 3145732
  77.3 2.5 copy-start.7
  79.8 2.1 copy-start.10
  79.9 2.1 copy-start.11
  79.9 2.1 copy-start.12
  79.9 2.9 copy-start.15
  84.2 54.9 %copy-start.8 = (bf16[512,512]{1,0:T(8,128)(2,1)S(1)}, bf16[512,512]{1,0:T(8,128)(2,1)}, u32[]{:S(2)}) copy-start(bf16[512,512]{1,0:T(8,128)(2,1)} %convolution_convert_fusion.8.query_ref) | copy-start | bytes 1572868
  184.6 1.7 copy-start.16
  194.8 102.7 %copy-start.4 = (bf16[512,1024]{1,0:T(8,128)(2,1)S(1)}, bf16[512,1024]{1,0:T(8,128)(2,1)}, u32[]{:S(2)}) copy-start(bf16[512,1024]{1,0:T(8,128)(2,1)} %param.29) | copy-start | bytes 3145732
  297.5 1.2 copy-start.3

commit v2 on v1

--- a/solution.py
+++ b/solution.py
@@ -28,15 +28,19 @@
     pl.semaphore_wait(barrier, n - 1)
 
 
-def remote(src, dst, send, recv, axis, peer):
+def remote_at(src, dst, send, recv, place):
     return pltpu.make_async_remote_copy(
         src_ref=src,
         dst_ref=dst,
         send_sem=send,
         recv_sem=recv,
-        device_id={axis: peer},
+        device_id=place,
         device_id_type=MESH,
     )
+
+
+def remote(src, dst, send, recv, axis, peer):
+    return remote_at(src, dst, send, recv, {axis: peer})
 
 
 def part(ref, dim, index, size):
@@ -514,9 +518,9 @@
 
 
 def chain_kernel(
-    n, layer, chunks, grads_ref, gates_ref, first_ref, query_ref, o_ref, other_ref,
+    n, layer, chunks, grads_ref, gates_ref, first_ref, query_ref, out_w_ref, o_ref, other_ref, far_w_ref,
     came, gates, state_in, state_out, stage, current,
-    send, recv, send_gate, recv_gate, send_back, recv_back, send_z, recv_z, send_q, recv_q,
+    send, recv, send_gate, recv_gate, send_back, recv_back, send_z, recv_z, send_q, recv_q, send_w, recv_w,
 ):
     me = lax.axis_index("seq")
     head = lax.axis_index("head")
@@ -561,6 +565,9 @@
         return remote(state_out.at[j], state_in.at[j], send_z.at[j], recv_z.at[j], "seq", up)
 
     query_copy = remote(query_ref, other_ref, send_q, recv_q, "head", 1 - head)
+    out_w_copy = remote(
+        part(out_w_ref, 1, 1 - head, far_w_ref.shape[1]), far_w_ref, send_w, recv_w, "head", 1 - head
+    )
 
     barrier = pltpu.get_barrier_semaphore()
     for k in range(1, layer):
@@ -580,6 +587,7 @@
     )
 
     query_copy.start()
+    out_w_copy.start()
     for k in range(1, layer):
         gate_copy(k).start()
 
@@ -661,9 +669,10 @@
     for k in range(1, layer):
         gate_copy(k).wait_send()
     query_copy.wait()
-
-
-def chain(grads, gates, first, query, identity):
+    out_w_copy.wait()
+
+
+def chain(grads, gates, first, query, out_w, identity):
     n = lax.axis_size("seq")
     layer = gates.shape[0]
     chunks = 16
@@ -674,9 +683,10 @@
         out_shape=(
             jax.ShapeDtypeStruct(grads.shape, jnp.bfloat16),
             jax.ShapeDtypeStruct(query.shape, jnp.bfloat16),
+            jax.ShapeDtypeStruct((out_w.shape[0], out_w.shape[1] // 2), jnp.bfloat16),
         ),
-        in_specs=[VMEM, VMEM, VMEM, VMEM],
-        out_specs=(VMEM, VMEM),
+        in_specs=[VMEM] * 5,
+        out_specs=(VMEM,) * 3,
         scratch_shapes=[
             pltpu.VMEM(part_of, jnp.bfloat16),
             pltpu.VMEM(gates.shape, jnp.float32),
@@ -692,11 +702,436 @@
             pltpu.SemaphoreType.DMA((chunks, layer)),
             pltpu.SemaphoreType.DMA((chunks,)),
             pltpu.SemaphoreType.DMA((chunks,)),
-            pltpu.SemaphoreType.DMA,
-            pltpu.SemaphoreType.DMA,
+            *[pltpu.SemaphoreType.DMA] * 4,
         ],
         compiler_params=pltpu.CompilerParams(collective_id=identity, has_side_effects=True),
-    )(grads, gates, first, query)
+    )(grads, gates, first, query, out_w)
+
+
+def greet(identity_axes):
+    barrier = pltpu.get_barrier_semaphore()
+    for place in identity_axes:
+        pl.semaphore_signal(barrier, inc=1, device_id=place, device_id_type=MESH)
+    pl.semaphore_wait(barrier, len(identity_axes))
+
+
+def swapped(x):
+    return pltpu.roll(x, HEAD_DIM, 1)
+
+
+def interleave(left, right, lane):
+    first = jnp.where(lane < HEAD_DIM, left, swapped(right))
+    second = jnp.where(lane < HEAD_DIM, swapped(left), right)
+    return narrow(first), narrow(second)
+
+
+def recall_kernel(
+    chunks, own_ref, other_ref, weights_ref, gain_ref, wq_ref, wk_ref, wv_ref, q_ref, kv_ref,
+    sent, came, kept, send, recv,
+):
+    head = lax.axis_index("head")
+    rows, half = own_ref.shape
+    width = 2 * half
+    piece = rows // chunks // 2
+    greet([{"head": 1 - head}])
+
+    def spans(i):
+        return (
+            pl.ds(pl.multiple_of(i * piece, piece), piece),
+            pl.ds(pl.multiple_of(rows // 2 + i * piece, piece), piece),
+        )
+
+    def exchange(i):
+        return remote(sent.at[i], came.at[i], send.at[i], recv.at[i], "head", 1 - head)
+
+    def retrieve(i, carry):
+        top, bottom = spans(i)
+        own = jnp.concatenate([own_ref[top, :], own_ref[bottom, :]], axis=0)
+        other = jnp.concatenate([other_ref[top, :], other_ref[bottom, :]], axis=0)
+        mine = weights_ref[pl.ds(pl.multiple_of(head * half, half), half), :]
+        theirs = weights_ref[pl.ds(pl.multiple_of((1 - head) * half, half), half), :]
+        pre_act = contract(own, mine, 1, 0) + contract(other, theirs, 1, 0)
+        hidden = narrow(pre_act * jax.nn.sigmoid(pre_act))
+        partial = contract(hidden, weights_ref[width:, :], 1, 1)
+        kept[i] = partial
+        sent[i] = narrow(partial)
+        exchange(i).start()
+        return carry
+
+    lax.fori_loop(0, chunks, retrieve, 0)
+    lane = lax.broadcasted_iota(jnp.int32, (piece, LANES), 1)
+    tall = lax.broadcasted_iota(jnp.int32, (2 * piece, LANES), 1)
+
+    def project_chunk(i, carry):
+        exchange(i).wait_recv()
+        top, bottom = spans(i)
+        retrieved = kept[i] + came[i].astype(jnp.float32)
+        mean_square = jnp.mean(retrieved * retrieved, axis=1, keepdims=True)
+        normed = narrow(retrieved * lax.rsqrt(mean_square + epsilon) * gain_ref[...])
+        query = contract(normed, wq_ref[...], 1, 0)
+        keys = contract(normed, wk_ref[...], 1, 0)
+        values = contract(normed, wv_ref[...], 1, 0)
+        for c in range(half // LANES):
+            columns = slice(c * LANES, (c + 1) * LANES)
+            left = slice(2 * c * LANES, (2 * c + 1) * LANES)
+            right = slice((2 * c + 1) * LANES, (2 * c + 2) * LANES)
+            q_ref[top, left], q_ref[top, right] = interleave(
+                query[:piece, columns], query[piece:, columns], lane
+            )
+            first, second = interleave(keys[:, columns], values[:, columns], tall)
+            kv_ref[top, left] = first[:piece]
+            kv_ref[bottom, left] = first[piece:]
+            kv_ref[top, right] = second[:piece]
+            kv_ref[bottom, right] = second[piece:]
+        return carry
+
+    lax.fori_loop(0, chunks, project_chunk, 0)
+
+    def finish(i, carry):
+        exchange(i).wait_send()
+        return carry
+
+    lax.fori_loop(0, chunks, finish, 0)
+
+
+def recall(own, other, weights, gain, wq, wk, wv, identity):
+    rows, half = own.shape
+    chunks = 4
+    part_of = (chunks, rows // chunks, 2 * half)
+    return pl.pallas_call(
+        functools.partial(recall_kernel, chunks),
+        out_shape=(
+            jax.ShapeDtypeStruct((rows // 2, 2 * half), jnp.bfloat16),
+            jax.ShapeDtypeStruct((rows, 2 * half), jnp.bfloat16),
+        ),
+        in_specs=[VMEM] * 7,
+        out_specs=(VMEM, VMEM),
+        scratch_shapes=[
+            pltpu.VMEM(part_of, jnp.bfloat16),
+            pltpu.VMEM(part_of, jnp.bfloat16),
+            pltpu.VMEM(part_of, jnp.float32),
+            pltpu.SemaphoreType.DMA((chunks,)),
+            pltpu.SemaphoreType.DMA((chunks,)),
+        ],
+        compiler_params=pltpu.CompilerParams(collective_id=identity, has_side_effects=True),
+    )(own, other, weights, gain, wq, wk, wv)
+
+
+def window_kernel(
+    n, heads, split, q_ref, kv_ref, near_w_ref, far_w_ref, o_ref,
+    q_all, kv_all, ctx, ctx_in, peaks, totals, w_top, w_bottom,
+    q_send, q_recv, kv_send, kv_recv, ctx_send, ctx_recv,
+):
+    me = lax.axis_index("seq")
+    plane = lax.axis_index("head")
+    chunk = me // heads
+    head = lax.rem(me, heads)
+    other = lax.rem(me + 1, n)
+    piece = q_ref.shape[0]
+
+    def ranges(which):
+        early = which == 0
+        first = jnp.where(early, 0, split)
+        last = jnp.where(early, split, n)
+        oldest = jnp.where(early, 0, split - SPAN)
+        return first, last, oldest
+
+    q_first, q_last, kv_first = ranges(chunk)
+    near_first = chunk * heads
+    tiles = q_last - q_first
+
+    def lanes(ref, which):
+        return ref.at[:, pl.ds(pl.multiple_of(which * LANES, LANES), LANES)]
+
+    def outgoing(peer):
+        first, last, oldest = ranges(peer // heads)
+        peer_head = lax.rem(peer, heads)
+        wants_kv = jnp.logical_and(me >= oldest, me < last)
+        wants_q = jnp.logical_and(me >= first, me < last)
+        slot = jnp.where(wants_kv, me - oldest, 0)
+        tile = jnp.where(wants_q, me - first, 0)
+        kv_copy = remote(
+            lanes(kv_ref, peer_head), kv_all.at[slot], kv_send.at[peer], kv_recv.at[slot], "seq", peer
+        )
+        q_copy = remote(
+            lanes(q_ref, peer_head), q_all.at[tile], q_send.at[peer], q_recv.at[tile], "seq", peer
+        )
+        return wants_kv, wants_q, kv_copy, q_copy
+
+    def peers(act):
+        def near(k, carry):
+            act(chunk * heads + lax.rem(head + k, heads))
+            return carry
+
+        def far(k, carry):
+            act((1 - chunk) * heads + lax.rem(head + k, heads))
+            return carry
+
+        lax.fori_loop(1, heads, near, 0)
+        lax.fori_loop(0, heads, far, 0)
+
+    def start_to(peer):
+        wants_kv, wants_q, kv_copy, q_copy = outgoing(peer)
+
+        @pl.when(wants_kv)
+        def _():
+            kv_copy.start()
+
+        @pl.when(wants_q)
+        def _():
+            q_copy.start()
+
+    def drain_to(peer):
+        wants_kv, wants_q, kv_copy, q_copy = outgoing(peer)
+
+        @pl.when(wants_kv)
+        def _():
+            kv_copy.wait_send()
+
+        @pl.when(wants_q)
+        def _():
+            q_copy.wait_send()
+
+    greet(
+        [{"seq": lax.rem(me + k, n), "head": plane} for k in range(1, n)]
+        + [{"seq": lax.rem(me + k, n), "head": 1 - plane} for k in range(n)]
+    )
+    peers(start_to)
+
+    own_columns = pl.ds(pl.multiple_of(head * LANES, LANES), LANES)
+    kv_all[me - kv_first] = kv_ref[:, own_columns]
+
+    @pl.when(jnp.logical_and(me >= q_first, me < q_last))
+    def _():
+        q_all[me - q_first] = q_ref[:, own_columns]
+
+    w_top[...] = jnp.zeros_like(w_top)
+    w_bottom[...] = jnp.zeros_like(w_bottom)
+
+    def spread(h, carry):
+        source = pl.ds(pl.multiple_of(h * HEAD_DIM, HEAD_DIM), HEAD_DIM)
+        for ref, side in ((near_w_ref, plane), (far_w_ref, 1 - plane)):
+            start = (side * heads + h) * LANES
+            w_top[pl.ds(pl.multiple_of(start, HEAD_DIM), HEAD_DIM), :] = ref[source, :]
+            w_bottom[pl.ds(pl.multiple_of(start + HEAD_DIM, HEAD_DIM), HEAD_DIM), :] = ref[source, :]
+        return carry
+
+    lax.fori_loop(0, heads, spread, 0)
+
+    def await_kv(block):
+        @pl.when(block != me)
+        def _():
+            slot = block - kv_first
+            remote(
+                kv_all.at[slot], kv_all.at[slot], kv_send.at[0], kv_recv.at[slot], "seq", other
+            ).wait_recv()
+
+    row = lax.broadcasted_iota(jnp.int32, (piece, 2 * piece), 0)
+    column = lax.broadcasted_iota(jnp.int32, (piece, 2 * piece), 1)
+    lane = lax.broadcasted_iota(jnp.int32, (piece, LANES), 1)
+    scale = math.log2(math.e) * HEAD_DIM**-0.5
+
+    def queries(tile):
+        packed = q_all[tile].astype(jnp.float32)
+        top = narrow(jnp.where(lane < HEAD_DIM, packed, 0.0))
+        bottom = narrow(jnp.where(lane < HEAD_DIM, swapped(packed), 0.0))
+        return top, bottom
+
+    def valued(pair):
+        place = lax.broadcasted_iota(jnp.int32, pair.shape, 1)
+        return jnp.where(place < HEAD_DIM, jnp.ones_like(pair), pair)
+
+    def scored(query, pair):
+        return contract(query, pair, 1, 1) * scale
+
+    def absorb(peak, total, scores, apply):
+        new_peak = jnp.maximum(peak, jnp.max(scores, axis=1, keepdims=True))
+        wide = jnp.concatenate([new_peak] * (2 * piece // LANES), axis=1)
+        weights = narrow(jnp.exp2(scores - wide))
+        return new_peak, total * jnp.exp2(peak - new_peak) + apply(weights)
+
+    def visit(tile, first, last, state):
+        query = queries(tile)
+
+        def whole(block, state):
+            pair = kv_all[block - kv_first]
+            values = valued(pair)
+            fresh = []
+            for part_query, (peak, total) in zip(query, state):
+                fresh.append(absorb(
+                    peak, total, scored(part_query, pair), lambda w: contract(w, values, 1, 0)
+                ))
+            return tuple(fresh)
+
+        return lax.fori_loop(first, last, whole, state)
+
+    def saved(tile):
+        return tuple((peaks[tile, i], totals[tile, i]) for i in range(2))
+
+    def context_copy(tile, side):
+        return remote_at(
+            ctx.at[tile], ctx_in.at[plane * heads + head], ctx_send.at[tile, side],
+            ctx_recv.at[plane * heads + head], {"seq": q_first + tile, "head": lax.rem(plane + side, 2)},
+        )
+
+    def near(tile, carry):
+        block = q_first + tile
+
+        @pl.when(block != me)
+        def _():
+            remote(
+                q_all.at[tile], q_all.at[tile], q_send.at[0], q_recv.at[tile], "seq", other
+            ).wait_recv()
+
+        def arrive(b, carry):
+            await_kv(b)
+            return carry
+
+        lax.fori_loop(jnp.where(tile == 0, near_first, block - 1), block, arrive, 0)
+        empty = (jnp.full((piece, LANES), -1e30, jnp.float32), jnp.zeros((piece, LANES), jnp.float32))
+        state = visit(tile, jnp.maximum(block - SPAN + 1, near_first), block, (empty, empty))
+        for i, (peak, total) in enumerate(state):
+            peaks[tile, i] = peak
+            totals[tile, i] = total
+        return carry
+
+    def far(step, carry):
+        block = q_last - 1 - step
+        tile = block - q_first
+
+        @pl.when(step == 0)
+        def _():
+            await_kv(block)
+
+        @pl.when(jnp.logical_and(block >= SPAN, block - SPAN < near_first))
+        def _():
+            await_kv(block - SPAN)
+
+        state = visit(tile, jnp.maximum(block - SPAN + 1, 0), near_first, saved(tile))
+        query = queries(tile)
+        pair = kv_all[block - kv_first]
+        values = valued(pair)
+
+        def close(states):
+            top, bottom = (total / total[:, :1] for peak, total in states)
+            ctx[tile] = narrow(jnp.where(lane < HEAD_DIM, swapped(top), bottom))
+
+        @pl.when(block < SPAN)
+        def _():
+            states = []
+            for i, (part_query, (peak, total)) in enumerate(zip(query, state)):
+                seen = column <= row + i * piece
+                scores = jnp.where(seen, scored(part_query, pair), -1e30)
+                states.append(absorb(peak, total, scores, lambda w: contract(w, values, 1, 0)))
+            close(states)
+
+        @pl.when(block >= SPAN)
+        def _():
+            old_pair = kv_all[block - SPAN - kv_first]
+            old_values = valued(old_pair)
+            states = []
+            for i, (part_query, (peak, total)) in enumerate(zip(query, state)):
+                seen = column <= row + i * piece
+                scores = jnp.where(seen, scored(part_query, pair), scored(part_query, old_pair))
+
+                def apply(w):
+                    none = jnp.zeros_like(w)
+                    return contract(jnp.where(seen, w, none), values, 1, 0) + contract(
+                        jnp.where(seen, none, w), old_values, 1, 0
+                    )
+
+                states.append(absorb(peak, total, scores, apply))
+            close(states)
+
+        context_copy(tile, 1).start()
+
+        @pl.when(block != me)
+        def _():
+            context_copy(tile, 0).start()
+
+        @pl.when(block == me)
+        def _():
+            ctx_in[plane * heads + head] = ctx[tile]
+
+        return carry
+
+    lax.fori_loop(0, tiles, near, 0)
+    lax.fori_loop(0, tiles, far, 0)
+
+    keeper = jnp.where(me < split, 0, heads)
+
+    def gathered(h, carry):
+        for side in range(2):
+            slot = lax.rem(plane + side, 2) * heads + h
+
+            def wait():
+                remote(
+                    ctx_in.at[slot], ctx_in.at[slot], ctx_send.at[0, 0], ctx_recv.at[slot], "seq", other
+                ).wait_recv()
+
+            if side == 0:
+                pl.when(keeper + h != me)(wait)
+            else:
+                wait()
+        return carry
+
+    lax.fori_loop(0, heads, gathered, 0)
+    for side, weights in enumerate((w_top, w_bottom)):
+        total = jnp.zeros((piece, o_ref.shape[1]), jnp.float32)
+        for h in range(heads):
+            both = jnp.concatenate([ctx_in[2 * h], ctx_in[2 * h + 1]], axis=1)
+            total += contract(both, weights[2 * h * LANES : 2 * (h + 1) * LANES, :], 1, 0)
+        o_ref[side * piece : (side + 1) * piece, :] = narrow(total)
+
+    def sent(tile, carry):
+        context_copy(tile, 1).wait_send()
+
+        @pl.when(q_first + tile != me)
+        def _():
+            context_copy(tile, 0).wait_send()
+
+        return carry
+
+    lax.fori_loop(0, tiles, sent, 0)
+    peers(drain_to)
+
+
+def balance(n):
+    costs = [min(b, SPAN) + 1 for b in range(n)]
+    return min(range(SPAN, n), key=lambda s: max(sum(costs[:s]), sum(costs[s:])))
+
+
+def window(query, pairs, near_w, far_w, identity):
+    n = lax.axis_size("seq")
+    piece = query.shape[0]
+    heads = query.shape[1] // LANES
+    split = balance(n)
+    tiles = max(split, n - split)
+    slots = max(split, n - split + SPAN)
+    wide = (2 * heads * LANES, near_w.shape[1])
+    return pl.pallas_call(
+        functools.partial(window_kernel, n, heads, split),
+        out_shape=jax.ShapeDtypeStruct((2 * piece, near_w.shape[1]), jnp.bfloat16),
+        in_specs=[VMEM] * 4,
+        out_specs=VMEM,
+        scratch_shapes=[
+            pltpu.VMEM((tiles, piece, LANES), jnp.bfloat16),
+            pltpu.VMEM((slots, 2 * piece, LANES), jnp.bfloat16),
+            pltpu.VMEM((tiles, piece, LANES), jnp.bfloat16),
+            pltpu.VMEM((2 * heads, piece, LANES), jnp.bfloat16),
+            pltpu.VMEM((tiles, 2, piece, LANES), jnp.float32),
+            pltpu.VMEM((tiles, 2, piece, LANES), jnp.float32),
+            pltpu.VMEM(wide, jnp.bfloat16),
+            pltpu.VMEM(wide, jnp.bfloat16),
+            pltpu.SemaphoreType.DMA((n,)),
+            pltpu.SemaphoreType.DMA((tiles,)),
+            pltpu.SemaphoreType.DMA((n,)),
+            pltpu.SemaphoreType.DMA((slots,)),
+            pltpu.SemaphoreType.DMA((tiles, 2)),
+            pltpu.SemaphoreType.DMA((2 * heads,)),
+        ],
+        compiler_params=pltpu.CompilerParams(collective_id=identity, has_side_effects=True),
+    )(query, pairs, near_w, far_w)
 
 
 def paired_shards(
@@ -751,32 +1186,20 @@
     ]
     gates = jnp.pad(jnp.stack(chosen, axis=0), ((0, 5), (0, 0)))
     gates = gates.reshape(8, layer, LANES).transpose(1, 0, 2)
-    weights, query_other = chain(grads, gates, first, query_part, 3)
+    weights, query_other, far_w = chain(grads, gates, first, query_part, attn_out_w, 3)
+    att_query, att_pairs = recall(
+        query_part, query_other, weights, norm_gain[None, :], attn_query_w, attn_key_w, attn_value_w, 4
+    )
     half = query_part.shape[1]
-    mem_query = jnp.where(
-        my_head == 0,
-        jnp.concatenate([query_part, query_other], axis=1),
-        jnp.concatenate([query_other, query_part], axis=1),
-    )
-    query_hidden = narrow(jax.nn.silu(contract(mem_query, weights[:width], 1, 0)))
-    partial = narrow(contract(query_hidden, weights[width:], 1, 1))
-    normed = normalize(whole_sum(partial, "head", 4), norm_gain)
-    query_w = paired(attn_query_w, jnp.zeros_like(attn_query_w))
-    pair_w = paired(attn_key_w, attn_value_w)
-    att_query = narrow(contract(normed, query_w, 1, 0))
-    att_pairs = narrow(contract(normed, pair_w, 1, 0))
-    context = attend(att_query, att_pairs, 6)
-    heads = attn_out_w.shape[0] // HEAD_DIM
-    out_rows = attn_out_w.reshape(heads, HEAD_DIM, width)
-    out_w = jnp.concatenate([jnp.zeros_like(out_rows), out_rows], axis=1).reshape(
-        heads * LANES, width
-    )
-    return narrow(scatter_sum(narrow(contract(context, out_w, 1, 0)), "head", 1, 7))
+    near_w = lax.dynamic_slice_in_dim(attn_out_w, my_head * half, half, 1)
+    return window(att_query, att_pairs, near_w, far_w, 6)
 
 
 def fits(n_seq, n_head, units):
     layer = units // n_head // LANES
-    return n_head == 2 and layer * LANES * n_head == units and layer > 1 and n_seq % layer == 0
+    heads = units // n_head // HEAD_DIM
+    split_well = layer * LANES * n_head == units and layer > 1 and n_seq % layer == 0
+    return n_head == 2 and split_well and heads == SPAN and n_seq == 2 * heads
 
 
 def solution(mesh):

time: 324 us -> 267 us (0.82)
  the two profiles are of different devices: /device:TPU:27 before, /device:TPU:0 now
where the time goes in v2:
time: 267 us; the launch traced here: 266 us
  Pallas kernels  230 us (86%)
  matrix products  17.9 us (7%)
  local copies, waits for them, and re-layouts  10.2 us (4%)
  other arithmetic  7.18 us (3%)
    pallas_call x1, Pallas kernels, window(): pl.pallas_call(functools.partial(window_kernel, n, heads, split), out_sha...  91.5 us
    pallas_call x1, Pallas kernels, chain(): pl.pallas_call(functools.partial(chain_kernel, n, layer, chunks), out_sha...  54.9 us
    pallas_call x2, Pallas kernels, comm_call(): pl.pallas_call(kernel, out_shape=out, in_specs=[ANY], out_specs=ANY, scra...  52.9 us
    pallas_call x1, Pallas kernels, recall(): pl.pallas_call(functools.partial(recall_kernel, chunks), out_shape=(jax.S...  30.9 us
    dot_general x7, matrix products, contract(): lax.dot_general(left, right, (((left_dim,), (right_dim,)), ((), ())), pre...  17.9 us
    unnamed x28, local copies, waits for them, and re-layouts  5.62 us

profile of v2, /device:TPU:0, one launch (start us, length us, event | category | flops | bytes accessed | tf_op | source)
XLA Modules:
  0.0 266.2 jit_solution(11763569754462100969)
XLA Ops:
  0.0 0.0 copy-start
  0.0 1.2 copy-done
  1.2 2.7 %convolution_convert_fusion.4.query_ref.own_ref = bf16[512,512]{1,0:T(8,128)(2,1)} fusion(bf16[512,1024]{1,0:T(8,128)(2,1)S(1)} %copy-done, bf16[1024,512]{1,0:T(8,128)(2,1)} %param.16), kind=kOutput, calls=%fused_computation.12 | convolution fusion | flops 537133056 | bytes 2621440 | tf_op jit(solution)/shard_map/dot_general | solution.py:417
  4.0 1.6 broadcast_in_dim.27
  5.5 0.0 copy-done.11
  5.5 1.7 fusion.2
  7.2 1.5 convolution_convert_fusion.3.x_ref
  8.7 20.0 %shard_map.145 = bf16[512,1024]{1,0:T(8,128)(2,1)} custom-call(bf16[512,512]{1,0:T(8,128)(2,1)} %convolution_convert_fusion.3.x_ref), custom_call_target="tpu_custom_call" | custom-call | tf_op jit(solution)/shard_map/pallas_call | solution.py:91
  28.8 0.0 copy-start.7
  28.8 2.1 fusion.7
  30.9 0.0 copy-start.5
  30.9 1.0 copy-done.5
  31.9 3.3 %subtract_convert_fusion.x_ref = bf16[512,1024]{1,0:T(8,128)(2,1)} fusion(f32[512,1024]{1,0:T(8,128)} %fusion.2, f32[512,1024]{1,0:T(8,128)S(1)} %copy-done.7, f32[512,512]{1,0:T(8,128)S(1)} %fusion.7), kind=kOutput, calls=%fused_computation.3 | convolution fusion | flops 539754496 | bytes 6291456 | tf_op jit(solution)/shard_map/dot_general | solution.py:417
  35.2 32.9 %shard_map.146 = bf16[1024,1024]{1,0:T(8,128)(2,1)} custom-call(bf16[512,1024]{1,0:T(8,128)(2,1)} %subtract_convert_fusion.x_ref), custom_call_target="tpu_custom_call" | custom-call | tf_op jit(solution)/shard_map/pallas_call | solution.py:91
  68.1 0.0 copy-start.6
  68.1 2.4 convert_reduce_fusion
  70.5 1.3 copy-done.4
  71.8 1.8 convolution_convert_fusion
  73.7 4.7 %convolution_convert_fusion.1 = bf16[1024,512]{1,0:T(8,128)(2,1)} fusion(bf16[512,1024]{1,0:T(8,128)(2,1)S(1)} %copy-done.1, f32[512,512]{1,0:T(8,128)S(1)} %copy-done.6, f32[512,1024]{1,0:T(8,128)} %param.20, f32[512,1024]{1,0:T(8,128)} %copy-done.4), kind=kOutput, calls=%fused_computation.5 | convolution fusion | flops 1078198272 | bytes 7340032 | tf_op jit(solution)/shard_map/dot_general | solution.py:417
  78.4 3.0 %pad_maximum_fusion.grads_ref = bf16[2048,512]{1,0:T(8,128)(2,1)} fusion(bf16[1024,512]{1,0:T(8,128)(2,1)} %convolution_convert_fusion, bf16[1024,512]{1,0:T(8,128)(2,1)} %convolution_convert_fusion.1), kind=kLoop, calls=%fused_computation.1 | loop fusion | flops 4194304 | bytes 4194304 | tf_op jit(solution)/shard_map/concatenate | solution.py:1175
  82.1 0.1 select_reduce_fusion.2
  82.2 0.6 fusion.13.gates_ref
  82.8 1.1 constant_dynamic-slice_fusion.1
  83.9 0.2 copy.17
  84.1 1.1 constant_dynamic-slice_fusion.2
  85.2 1.1 pad_maximum_fusion.1.first_ref
  86.2 54.9 %shard_map.147 = (bf16[2048,512]{1,0:T(8,128)(2,1)}, bf16[512,512]{1,0:T(8,128)(2,1)}, bf16[512,512]{1,0:T(8,128)(2,1)}) custom-call(bf16[2048,512]{1,0:T(8,128)(2,1)} %pad_maximum_fusion.grads_ref, f32[4,8,128]{2,1,0:T(8,128)} %fusion.13.gates_ref, f32[2048,128]{1,0:T(8,128)} %pad_maximum_fusion.1.first_ref, ...), custom_call_target="tpu_custom_call" | custom-call | tf_op jit(solution)/shard_map/pallas_call | solution.py:681
  141.1 0.0 copy-start.3
  141.1 30.9 %shard_map.148 = (bf16[256,1024]{1,0:T(8,128)(2,1)}, bf16[512,1024]{1,0:T(8,128)(2,1)}) custom-call(bf16[512,512]{1,0:T(8,128)(2,1)} %convolution_convert_fusion.4.query_ref.own_ref, bf16[512,512]{1,0:T(8,128)(2,1)} %get-tuple-element.10.other_ref, bf16[2048,512]{1,0:T(8,128)(2,1)} %get-tuple-element.11.weights_ref, f32[1,1024]{1,0:T(1,128)} %bitcast.26, ...), custom_call_target="tpu_custom_call" | custom-call | tf_op jit(solution)/shard_map/pallas_call | solution.py:801
  172.0 0.8 constant_dynamic-slice_fusion.near_w_ref
  172.9 91.5 %shard_map.149 = bf16[512,512]{1,0:T(8,128)(2,1)} custom-call(bf16[256,1024]{1,0:T(8,128)(2,1)} %get-tuple-element.12.q_ref, bf16[512,1024]{1,0:T(8,128)(2,1)} %get-tuple-element.13.kv_ref, bf16[512,512]{1,0:T(8,128)(2,1)} %constant_dynamic-slice_fusion.near_w_ref, bf16[512,512]{1,0:T(8,128)(2,1)} %get-tuple-element.14.far_w_ref), custom_call_target="tpu_custom_call" | custom-call | tf_op jit(solution)/shard_map/pallas_call | solution.py:1112
  264.3 1.9 copy.21
  (18 shorter events, 0.0 us)
Async XLA Ops:
  0.0 1.2 copy-start
  0.0 5.5 %copy-start.11 = (bf16[1024,512]{1,0:T(8,128)(2,1)S(1)}, bf16[1024,512]{1,0:T(8,128)(2,1)}, u32[]{:S(2)}) copy-start(bf16[1024,512]{1,0:T(8,128)(2,1)} %param.18) | copy-start | bytes 3145732
  5.5 1.7 copy-start.12
  7.2 21.5 %copy-start.2 = (f32[1024,512]{1,0:T(8,128)S(1)}, f32[1024,512]{1,0:T(8,128)}, u32[]{:S(2)}) copy-start(f32[1024,512]{1,0:T(8,128)} %param.19) | copy-start | bytes 6291460
  28.8 3.1 %copy-start.7 = (f32[512,1024]{1,0:T(8,128)S(1)}, f32[512,1024]{1,0:T(8,128)}, u32[]{:S(2)}) copy-start(f32[512,1024]{1,0:T(8,128)} %param.20) | copy-start | bytes 6291460
  30.9 1.0 copy-start.5
  68.1 3.7 %copy-start.6 = (f32[512,512]{1,0:T(8,128)S(1)}, f32[512,512]{1,0:T(8,128)}, u32[]{:S(2)}) copy-start(f32[512,512]{1,0:T(8,128)} %copy-done.5) | copy-start | bytes 3145732
  70.5 1.3 copy-start.4
  71.8 1.8 copy-start.1
  78.4 3.7 %copy-start.8 = (f32[16,512]{1,0:T(8,128)S(1)}, f32[16,512]{1,0:T(8,128)}, u32[]{:S(2)}) copy-start(f32[16,512]{1,0:T(8,128)} %param.22) | copy-start | bytes 98308
  78.4 3.7 %copy-start.9 = (f32[16,512]{1,0:T(8,128)S(1)}, f32[16,512]{1,0:T(8,128)}, u32[]{:S(2)}) copy-start(f32[16,512]{1,0:T(8,128)} %param.21) | copy-start | bytes 98308
  78.4 3.7 %copy-start.10 = (f32[16,512]{1,0:T(8,128)S(1)}, f32[16,512]{1,0:T(8,128)}, u32[]{:S(2)}) copy-start(f32[16,512]{1,0:T(8,128)} %param.23) | copy-start | bytes 98308
  141.1 30.9 %copy-start.3 = (bf16[512,1024]{1,0:T(8,128)(2,1)S(1)}, bf16[512,1024]{1,0:T(8,128)(2,1)}, u32[]{:S(2)}) copy-start(bf16[512,1024]{1,0:T(8,128)(2,1)} %out_w_ref.1) | copy-start | bytes 3145732
